TPU v7x, 32 devices: a whole 2x2x4 slice. The times are simulated.
32 devices in a mesh: fsdp: 32 (over z, y, x, core).
Axes of the slice: x: 2, y: 2, z: 4, core: 2. Of those that a mesh axis runs over, the one named last changes fastest.
Arguments:
- tok_ids: int32 [32, 128], P('fsdp')
- tok_labels: int32 [32, 128], P('fsdp')
- embed: bfloat16 [32128, 768], P('fsdp')
- w_gate: bfloat16 [768, 3072], P('fsdp')
- w_up: bfloat16 [768, 3072], P('fsdp')
- w_down: bfloat16 [3072, 768], P('fsdp')
- gain_mlp: float32 [768], replicated
- gain_final: float32 [768], replicated
Outputs:
- output 1: float32 [], replicated
- output 2: float32 [32128, 768], P('fsdp')
- output 3: float32 [768, 3072], P('fsdp')
- output 4: float32 [768, 3072], P('fsdp')
- output 5: float32 [3072, 768], P('fsdp')
All inputs are finite; a program needn't handle non-finite values.
Results may differ from a plain program's by a relative error of at most 0.0122675.
Values are sent between devices in bfloat16 or wider.
A program may use at most 1 GiB of HBM per device.

v0:
```python
import math
import jax
import jax.numpy as jnp
from jax import lax
from jax.experimental import pallas as pl
from jax.experimental.pallas import tpu as pltpu
from jax.sharding import PartitionSpec as P

NORM_EPS = 1e-6
MESH = pl.DeviceIdType.MESH
F32 = jnp.float32
BF16 = jnp.bfloat16
VMEM_CAP = 63 * 1024 * 1024
LANE = 128
DIM = 768
PAIR = 48
UNITS = 384
NDEV = 32
LEVEL = 8
HEIGHT = 4
DROWS = 96
CHIPS = 16
GROWS = 24
TWO = 2
TOP = 3
VSPEC = pl.BlockSpec(memory_space=pltpu.VMEM)
HSPEC = pl.BlockSpec(memory_space=pl.ANY)


def my_place():
    me = lax.axis_index('fsdp')
    core = lax.rem(me, TWO)
    x = lax.rem(lax.div(me, TWO), TWO)
    y = lax.rem(lax.div(me, HEIGHT), TWO)
    z = lax.div(me, LEVEL)
    p = x * (1 - core) + y * core
    q = y * (1 - core) + x * core
    return me, z, p, q, core


def chip_of(z, p, q, core):
    x = p * (1 - core) + q * core
    y = q * (1 - core) + p * core
    return (z * TWO + y) * TWO + x


def device_of(z, p, q, core):
    return chip_of(z, p, q, core) * TWO + core


def barrier_peers(place):
    me, z = place[0], place[1]
    sem = pltpu.get_barrier_semaphore()
    for step in range(1, LEVEL):
        dev = z * LEVEL + lax.rem(me + step, LEVEL)
        pl.semaphore_signal(sem, inc=1, device_id=(dev,), device_id_type=MESH)
    for step in range(1, HEIGHT):
        dev = lax.rem(me + LEVEL * step, NDEV)
        pl.semaphore_signal(sem, inc=1, device_id=(dev,), device_id_type=MESH)
    pl.semaphore_wait(sem, 10)


def far_level(z, at):
    half = lax.div(z, TWO)
    inner = lax.rem(z + half, TWO)
    order = (TOP - TOP * half, (1 - inner) * (TWO - half) + inner * TOP * half, 1 + lax.rem(z, TWO), z)
    if isinstance(at, int):
        return order[at]
    low, high = lax.rem(at, TWO), lax.div(at, TWO)
    return ((1 - low) * (1 - high) * order[0] + low * (1 - high) * order[1]
            + (1 - low) * high * order[TWO] + low * high * order[TOP])


def remote(src, dst, sems, slot, dev):
    return pltpu.make_async_remote_copy(
        src_ref=src, dst_ref=dst, send_sem=sems.at[0, slot], recv_sem=sems.at[1, slot],
        device_id=(dev,), device_id_type=MESH)


def sem_pair(n):
    return pltpu.SemaphoreType.DMA((TWO, n))


def gather_levels(in_ref, out_ref, send_sem, recv_sem, place, work, hook=None, late_hook=None):
    me, z, p, q, core = place
    peers = (me + LEVEL, me - LEVEL, device_of(z, 1 - p, q, core), device_of(z, p, 1 - q, core), me + 1 - TWO * core)

    def desc(block, way, src=None):
        return pltpu.make_async_remote_copy(
            src_ref=out_ref.at[block] if src is None else src, dst_ref=out_ref.at[block],
            send_sem=send_sem.at[slot(block, way)], recv_sem=recv_sem.at[block],
            device_id=(peers[way],), device_id_type=MESH)

    def slot(block, way):
        chip, lv = lax.div(block, TWO), lax.div(block, LEVEL)
        mid = lax.rem(chip, TWO) * (1 - core) + lax.rem(lax.div(chip, TWO), TWO) * core
        return (lv, HEIGHT + lv, LEVEL + lv, 12 + lv * TWO + mid, 20 + chip)[way]

    def got(block):
        desc(block, HEIGHT).wait_recv()

    pl.when(z < TOP)(lambda: desc(me, 0, in_ref).start())
    pl.when(z > 0)(lambda: desc(me, 1, in_ref).start())
    for way in (TOP, TWO, HEIGHT):
        desc(me, way, in_ref).start()
    out_ref[me] = in_ref[...]

    def take_z(level):
        block = device_of(level, p, q, core)
        got(block)
        pl.when(jnp.logical_and(level < z, z < TOP))(lambda: desc(block, 0).start())
        pl.when(jnp.logical_and(level > z, z > 0))(lambda: desc(block, 1).start())
        for way in (TOP, TWO, HEIGHT):
            desc(block, way).start()

    def take_p(level):
        block = device_of(level, 1 - p, q, core)
        got(block)
        for way in (TOP, HEIGHT):
            desc(block, way).start()

    y = q * (1 - core) + p * core

    def take_q(level, mid):
        block = device_of(level, mid, 1 - q, core)
        got(block)
        desc(block, HEIGHT).start()

    def take_half(level, row):
        for x in range(TWO):
            got(level * LEVEL + row * HEIGHT + x * TWO + 1 - core)
        work(level * LEVEL + row * HEIGHT)

    def take_level(level):
        pl.when(core == 1)(lambda: take_q(level, p))
        take_half(level, y)
        pl.when(core == 0)(lambda: take_q(level, p))
        take_q(level, 1 - p)
        take_half(level, 1 - y)

    def step(t, carry):
        if hook is not None:
            hook(t)
        pl.when(jnp.logical_or(t == 0, jnp.logical_and(t < TOP, outer)))(lambda: take_z(far_level(z, TWO - lax.rem(t, TOP))))
        pl.when(jnp.logical_and(t == 0, inner))(lambda: take_z(far_level(z, 1)))
        pl.when(jnp.logical_and(t > 0, t < HEIGHT))(lambda: take_p(far_level(z, TOP - lax.rem(t, HEIGHT))))
        pl.when(jnp.logical_and(t == 1, inner))(lambda: take_z(far_level(z, 0)))
        if late_hook is not None:
            late_hook(t)

        @pl.when(t > 0)
        def _():
            level = far_level(z, HEIGHT - (t + lax.div(HEIGHT - t, HEIGHT)))
            take_level(level)
        return carry

    outer = jnp.logical_or(z == 0, z == TOP)
    inner = jnp.logical_not(outer)
    take_p(z)
    lax.fori_loop(0, 5, step, 0)
    for level in range(HEIGHT):
        desc(device_of(level, p, q, core), TWO).wait_send()
        for mid in range(TWO):
            desc(device_of(level, mid, q, core), TOP).wait_send()
        pl.when(jnp.logical_and(z < TOP, level <= z))(lambda: desc(device_of(level, p, q, core), 0).wait_send())
        pl.when(jnp.logical_and(z > 0, level >= z))(lambda: desc(device_of(level, p, q, core), 1).wait_send())
    for chip in range(CHIPS):
        desc(chip * TWO + core, HEIGHT).wait_send()


def add_into(dst, srcs, rows):
    step = 32

    def body(i, carry):
        sl = pl.ds(pl.multiple_of(i * step, step), step)
        total = srcs[0][sl, :].astype(F32)
        for src in srcs[1:]:
            total = total + src[sl, :].astype(F32)
        dst[sl, :] = total.astype(dst.dtype)
        return carry

    lax.fori_loop(0, rows // step, body, 0)


def scatter_scratch(rows, cols):
    return [
        pltpu.VMEM((CHIPS, rows, cols), BF16), pltpu.VMEM((LEVEL, rows, cols), BF16), pltpu.VMEM((HEIGHT, rows, cols), BF16),
        pltpu.VMEM((HEIGHT, rows, cols), BF16), pltpu.VMEM((HEIGHT, rows, cols), BF16), pltpu.VMEM((CHIPS, rows, cols), BF16),
        pltpu.VMEM((rows, cols), F32),
        pltpu.SemaphoreType.DMA((TWO, CHIPS)), pltpu.SemaphoreType.DMA((TWO, LEVEL)), pltpu.SemaphoreType.DMA((TWO, HEIGHT)),
        pltpu.SemaphoreType.DMA((TWO, HEIGHT)), pltpu.SemaphoreType.DMA((TWO, HEIGHT)),
    ]


def scatter_levels(in_ref, out_ref, scratch, place, work, hook=None):
    from_core, from_q, from_p, from_low, from_high, outgo, acc, sem_c, sem_q, sem_p, sem_up, sem_dn = scratch
    me, z, p, q, core = place
    rows = out_ref.shape[0]
    other = 1 - core

    def core_copy(chip):
        return remote(in_ref.at[chip * TWO + other], from_core.at[chip], sem_c, chip, me + 1 - TWO * core)

    def local(level, mid, last):
        return level * HEIGHT + mid * TWO + last

    def q_copy(level, mid):
        return remote(outgo.at[local(level, mid, 1 - q)], from_q.at[level * TWO + mid], sem_q, level * TWO + mid,
                      device_of(z, p, 1 - q, core))

    def p_copy(level):
        return remote(outgo.at[local(level, 1 - p, q)], from_p.at[level], sem_p, level, device_of(z, 1 - p, q, core))

    def up_copy(level):
        return remote(outgo.at[local(level, p, q)], from_low.at[level], sem_up, level, me + LEVEL)

    def dn_copy(level):
        return remote(outgo.at[local(level, p, q)], from_high.at[level], sem_dn, level, me - LEVEL)

    def own(level, mid, last):
        chip = chip_of(level, mid, last, core)
        core_copy(chip).wait_recv()
        return [in_ref.at[chip * TWO + core], from_core.at[chip]]

    y = q * (1 - core) + p * core
    x = p * (1 - core) + q * core

    def make(level, half):
        row = level * HEIGHT + TWO * (y * half + (1 - y) * (1 - half))
        work(row * TWO)
        for side in (1 - x, x):
            core_copy(row + side).start()

    def send_q(level, mid):
        add_into(outgo.at[local(level, mid, 1 - q)], own(level, mid, 1 - q), rows)
        q_copy(level, mid).start()

    def send_p(level):
        side = own(level, 1 - p, q)
        q_copy(level, 1 - p).wait_recv()
        add_into(outgo.at[local(level, 1 - p, q)], side + [from_q.at[level * TWO + 1 - p]], rows)
        p_copy(level).start()

    def gather_here(level):
        mine = own(level, p, q)
        q_copy(level, p).wait_recv()
        p_copy(level).wait_recv()
        return mine + [from_q.at[level * TWO + p], from_p.at[level]]

    def send_z(level):
        add_into(acc, gather_here(level), rows)

        @pl.when(level > z)
        def _():
            @pl.when(z > 0)
            def _():
                up_copy(level).wait_recv()
                add_into(acc, [acc, from_low.at[level]], rows)
            add_into(outgo.at[local(level, p, q)], [acc], rows)
            up_copy(level).start()

        @pl.when(level < z)
        def _():
            @pl.when(z < TOP)
            def _():
                dn_copy(level).wait_recv()
                add_into(acc, [acc, from_high.at[level]], rows)
            add_into(outgo.at[local(level, p, q)], [acc], rows)
            dn_copy(level).start()

    def level_at(t):
        return far_level(z, lax.rem(lax.div(t, TWO), HEIGHT))

    def step(t, carry):
        odd = lax.rem(t, TWO)
        if hook is not None:
            hook(t)
        pl.when(t < LEVEL)(lambda: make(level_at(t), odd))
        pl.when(jnp.logical_and(t > 0, t < 9))(lambda: send_q(level_at(t + 7), odd * (1 - p) + (1 - odd) * p))
        pl.when(jnp.logical_and(t == 9, inner))(lambda: send_z(far_level(z, 1)))
        pl.when(jnp.logical_and(t > TWO, odd == 1))(lambda: send_p(level_at(t + 5)))
        pl.when(jnp.logical_and(jnp.logical_and(t > HEIGHT, odd == 1), outer))(lambda: send_z(level_at(t + TOP)))
        pl.when(jnp.logical_and(jnp.logical_and(t > 6, odd == 1), inner))(lambda: send_z(far_level(z, TWO * lax.div(t, 9))))
        return carry

    outer = jnp.logical_or(z == 0, z == TOP)
    inner = jnp.logical_not(outer)
    lax.fori_loop(0, 10, step, 0)
    add_into(out_ref, gather_here(z), rows)

    @pl.when(z > 0)
    def _():
        up_copy(z).wait_recv()
        add_into(out_ref, [out_ref, from_low.at[z]], rows)

    @pl.when(z < TOP)
    def _():
        dn_copy(z).wait_recv()
        add_into(out_ref, [out_ref, from_high.at[z]], rows)

    for chip in range(CHIPS):
        core_copy(chip).wait_send()
    for level in range(HEIGHT):
        for mid in range(TWO):
            q_copy(level, mid).wait_send()
        p_copy(level).wait_send()
        pl.when(level > z)(lambda: up_copy(level).wait_send())
        pl.when(level < z)(lambda: dn_copy(level).wait_send())


def rank_of(p, q, core):
    return device_of(0, p, q, core)


def level_gather(in_ref, out_ref, send_sem, recv_sem, place):
    me, z, p, q, core = place
    rank = lax.rem(me, LEVEL)
    peers = (device_of(z, 1 - p, q, core), device_of(z, p, 1 - q, core), me + 1 - TWO * core)

    def desc(block, way, src=None):
        return pltpu.make_async_remote_copy(
            src_ref=out_ref.at[block] if src is None else src, dst_ref=out_ref.at[block],
            send_sem=send_sem.at[(0, 1 if src is not None else TWO, TOP + lax.div(block, TWO))[way]], recv_sem=recv_sem.at[block],
            device_id=(peers[way],), device_id_type=MESH)

    for way in (1, 0, TWO):
        desc(rank, way, in_ref).start()
    out_ref[rank] = in_ref[...]
    side = rank_of(1 - p, q, core)
    desc(side, 0).wait_recv()
    for way in (1, TWO):
        desc(side, way).start()
    for mid in (p, 1 - p):
        block = rank_of(mid, 1 - q, core)
        desc(block, 1).wait_recv()
        desc(block, TWO).start()
    for chip in range(HEIGHT):
        desc(chip * TWO + 1 - core, TWO).wait_recv()
    desc(rank, 0, in_ref).wait_send()
    desc(rank, 1, in_ref).wait_send()
    desc(side, 1).wait_send()
    for chip in range(HEIGHT):
        desc(chip * TWO + core, TWO).wait_send()


def level_scatter(in_ref, out_ref, from_core, from_q, from_p, outgo, sem_s, sem_r, place, hook=None):
    me, z, p, q, core = place
    rows = out_ref.shape[0]

    def copy(src, dst, slot, dev):
        return pltpu.make_async_remote_copy(
            src_ref=src, dst_ref=dst, send_sem=sem_s.at[slot], recv_sem=sem_r.at[slot],
            device_id=(dev,), device_id_type=MESH)

    def core_copy(chip):
        return copy(in_ref.at[chip * TWO + 1 - core], from_core.at[chip], chip, me + 1 - TWO * core)

    def q_copy(mid):
        return copy(outgo.at[mid], from_q.at[mid], HEIGHT + mid, device_of(z, p, 1 - q, core))

    def p_copy():
        return copy(outgo.at[TWO], from_p, 6, device_of(z, 1 - p, q, core))

    def own(mid, last):
        chip = chip_of(0, mid, last, core)
        core_copy(chip).wait_recv()
        return [in_ref.at[chip * TWO + core], from_core.at[chip]]

    for last in (1 - p, p):
        for mid in (1 - q, q):
            core_copy(chip_of(0, mid, last, 1 - core)).start()
    for mid in (1 - p, p):
        add_into(outgo.at[mid], own(mid, 1 - q), rows)
        q_copy(mid).start()
    if hook is not None:
        hook()
    side = own(1 - p, q)
    q_copy(1 - p).wait_recv()
    add_into(outgo.at[TWO], side + [from_q.at[1 - p]], rows)
    p_copy().start()
    mine = own(p, q)
    q_copy(p).wait_recv()
    p_copy().wait_recv()
    add_into(out_ref, mine + [from_q.at[p], from_p], rows)
    for chip in range(HEIGHT):
        core_copy(chip).wait_send()
    for mid in range(TWO):
        q_copy(mid).wait_send()
    p_copy().wait_send()


def dot(left, right, ld, rd):
    return lax.dot_general(left, right, (((ld,), (rd,)), ((), ())), preferred_element_type=F32)


TOKS = 512
VPAD = 1024
VROWS = 1004


def id_rows(tok_ref, row, first):
    ids = jnp.concatenate([tok_ref[first + t, row:row + 1, :] for t in range(HEIGHT)], axis=1) - shard_start()
    return jnp.where(jnp.logical_and(ids >= 0, ids < VROWS), ids, -1)


def vocab_iota():
    return lax.broadcasted_iota(jnp.int32, (VPAD, TOKS), 0)


def shard_start():
    return lax.axis_index('fsdp') * VROWS


def fill_table(table, emb_ref):
    table[VPAD - 32:VPAD, :] = jnp.zeros((32, DIM), BF16)
    table[0:VROWS, :] = emb_ref[...]


def rms_inv(values):
    return lax.rsqrt(jnp.mean(values * values, axis=-1, keepdims=True) + NORM_EPS)


def rms_backward(values, inv_rms, gain_vec, grad_out):
    scaled = grad_out * gain_vec
    return inv_rms * scaled - values * (inv_rms ** TOP) * jnp.mean(scaled * values, axis=-1, keepdims=True)


LEVEL_SCRATCH = [
    pltpu.VMEM((LANE, DIM), BF16), pltpu.VMEM((LEVEL, LANE, DIM), BF16), pltpu.VMEM((LANE, DIM), F32),
    pltpu.VMEM((HEIGHT, LANE, DIM), BF16), pltpu.VMEM((TWO, LANE, DIM), BF16), pltpu.VMEM((LANE, DIM), BF16),
    pltpu.VMEM((TOP, LANE, DIM), BF16),
    pltpu.SemaphoreType.DMA((7,)), pltpu.SemaphoreType.DMA((LEVEL,)),
    pltpu.SemaphoreType.DMA((7,)), pltpu.SemaphoreType.DMA((7,)),
]


def split_weights(gu_ref):
    wide = gu_ref[...].astype(F32)
    return (wide[:, 0:GROWS, :].reshape(DIM, UNITS).astype(BF16), wide[:, GROWS:PAIR, :].reshape(DIM, UNITS).astype(BF16))


GU_SHAPE = (NDEV, PAIR, UNITS)
WD_SHAPE = (HEIGHT, DROWS, DIM)


def call(kernel, name, cid, outs, ins, scratch):
    return pl.pallas_call(
        kernel, out_shape=outs, in_specs=[VSPEC if i != TWO else HSPEC for i in range(len(ins))],
        out_specs=(HSPEC,) * (len(outs) - 1) + (pl.BlockSpec(memory_space=pltpu.SMEM),),
        scratch_shapes=scratch,
        compiler_params=pltpu.CompilerParams(collective_id=cid, has_side_effects=True, vmem_limit_bytes=VMEM_CAP),
        name=name)(*ins)


STAT = 40


def merge_stats(blocks):
    logs = [b[0:32, :] for b in blocks]
    top = logs[0]
    for one in logs[1:]:
        top = jnp.maximum(top, one)
    total = jnp.exp(logs[0] - top)
    labs = blocks[0][32:STAT, :]
    for one, b in zip(logs[1:], blocks[1:]):
        total = total + jnp.exp(one - top)
        labs = labs + b[32:STAT, :]
    return jnp.concatenate([top + jnp.log(total), labs], axis=0)


def step_call(ids, labs, emb, gate, up, down_shard, gain_mlp, gain_final, emb_scale, inv_count):
    def kernel(ids_ref, lab_ref, emb_ref, gate_ref, up_ref, down_ref, gm_ref, gf_ref,
               demb_out, dgate_out, dup_out, dn_out, loss_ref,
               demb_ref, dgate_ref, dup_ref, dn_ref, emb_in, sem_o, piece_ref, own_ref, tok_mine, tok_ref, table, spread, whole, gu_ref, wd_ref, a_ref, g_ref, u_ref, dm_ref,
               d_gate, d_up, acts, grad_gate, grad_up, grad_down, ggu, gd, land_g, land_d, outgo, outgo_d, acc,
               block, x_ref, h_ref, dh_ref, dhn_ref, stat, land, land_z, lse_ref,
               sem_t, sem_a, g_send, g_recv, sem_z, sem_d,
               *scratch):
        ring, (mine, parts, total, *level) = scratch[:12], scratch[12:]
        place = my_place()
        me, z, p, q, core = place
        rank = lax.rem(me, LEVEL)
        gain_m, gain_f = gm_ref[...].reshape(1, DIM), gf_ref[...].reshape(1, DIM)
        table_in = pltpu.make_async_copy(emb_ref, emb_in, sem_o.at[11])
        table_in.start()
        tok_mine[...] = jnp.zeros((LEVEL, LANE), jnp.int32)
        tok_mine[0:1, :] = ids_ref[...]
        tok_mine[1:TWO, :] = lab_ref[...]
        both = jnp.concatenate([gate_ref[...].astype(F32), up_ref[...].astype(F32)], axis=0).astype(BF16)
        for r in range(LEVEL):
            piece_ref[r] = jnp.concatenate([both[:, DROWS * (LEVEL * k + r):DROWS * (LEVEL * k + r + 1)] for k in range(HEIGHT)], axis=1)
        barrier_peers(place)

        def exchange(step):
            peer = lax.rem(rank + step, LEVEL)
            return remote(piece_ref.at[peer], gu_ref.at[me], sem_a, step, z * LEVEL + peer)

        def rows_of(ref, lv):
            return ref.at[pl.ds(lv * LEVEL, LEVEL)]

        def slab(lv, way):
            part = rows_of(gu_ref, lv)
            return pltpu.make_async_remote_copy(
                src_ref=part, dst_ref=part, send_sem=sem_z.at[0, way * HEIGHT + lv], recv_sem=sem_z.at[1, lv],
                device_id=(me + LEVEL - CHIPS * way,), device_id_type=MESH)

        def slab_down(lv, way, src):
            return pltpu.make_async_remote_copy(
                src_ref=src, dst_ref=wd_ref.at[lv], send_sem=sem_d.at[0, way * HEIGHT + lv], recv_sem=sem_d.at[1, lv],
                device_id=(me + LEVEL - CHIPS * way,), device_id_type=MESH)

        def tell(step):
            return remote(tok_mine, tok_ref.at[me], sem_t, step, z * LEVEL + lax.rem(rank + step, LEVEL))

        def along_z(src, dst, sems, step):
            return remote(src, dst, sems, 7 + step, lax.rem(me + LEVEL * step, NDEV))

        for step in range(1, LEVEL):
            tell(step).start()
        tok_ref[me] = tok_mine[...]
        wd_ref[z] = down_ref[...]
        gu_ref[me] = piece_ref[rank]
        table_in.wait()
        fill_table(table, emb_in)
        stat[...] = jnp.zeros_like(stat)
        demb_ref[...] = jnp.zeros_like(demb_ref)
        for step in range(1, LEVEL):
            tell(step).wait()
        part = rows_of(tok_ref, z)
        for step in range(1, HEIGHT):
            along_z(part, part, sem_t, step).start()
        for step in range(1, LEVEL):
            exchange(step).start()
        pl.when(z < TOP)(lambda: slab_down(z, 0, down_ref).start())
        pl.when(z > 0)(lambda: slab_down(z, 1, down_ref).start())
        for step in range(1, HEIGHT):
            along_z(part, part, sem_t, step).wait()
        for step in range(1, LEVEL):
            exchange(step).wait_recv()
        pl.when(z < TOP)(lambda: slab(z, 0).start())
        pl.when(z > 0)(lambda: slab(z, 1).start())

        def take(lv, way, more):
            slab_down(lv, 0, wd_ref.at[lv]).wait_recv()
            pl.when(more)(lambda: slab_down(lv, way, wd_ref.at[lv]).start())
            slab(lv, 0).wait_recv()
            pl.when(more)(lambda: slab(lv, way).start())

        def take_far(far):
            pl.when(z - far >= 0)(lambda: take(z - far, 0, z < TOP))
            pl.when(z + far < HEIGHT)(lambda: take(z + far, 1, z > 0))

        def hit_rows(first):
            return (vocab_iota() == id_rows(tok_ref, 0, first)).astype(F32).astype(BF16)

        def find(first):
            spread[pl.ds(first, HEIGHT)] = dot(hit_rows(first), table[...], 0, 0).astype(BF16).reshape(HEIGHT, LANE, DIM)

        scatter_levels(spread, x_ref, ring, place, find, lambda t: pl.when(t == 6)(lambda: take_far(1)))
        take_far(TWO)
        x = x_ref[...] * emb_scale
        mine[...] = (x * rms_inv(x) * gain_m).astype(BF16)
        level_gather(mine, a_ref, level[HEIGHT], level[5], place)
        take_far(TOP)
        for half in range(TWO):
            four = slice(HEIGHT * half, HEIGHT * half + HEIGHT)
            wg, wu = split_weights(gu_ref)
            act_in = a_ref[four].reshape(TOKS, DIM)
            g = dot(act_in, wg, 1, 0).astype(BF16)
            u = dot(act_in, wu, 1, 0).astype(BF16)
            g_ref[half] = g
            u_ref[half] = u
            act = (jax.nn.silu(g.astype(F32)) * u.astype(F32)).astype(BF16)
            acts[half] = act
            parts[four] = dot(act, wd_ref[...].reshape(UNITS, DIM), 1, 0).astype(BF16).reshape(HEIGHT, LANE, DIM)
        level_scatter(parts, total, *level[:HEIGHT], *level[6:], place)
        h_ref[...] = (x_ref[...] * emb_scale + total[...].astype(BF16).astype(F32)).astype(BF16)
        h32 = h_ref[...].astype(F32)
        block[...] = (h32 * rms_inv(h32) * gain_f).astype(BF16)
        for step in range(1, LEVEL):
            exchange(step).wait_send()

        def sent(lv, way):
            slab(lv, way).wait_send()
            slab_down(lv, way, wd_ref.at[lv]).wait_send()

        def forward(first):
            logits = dot(table[...], whole[pl.ds(first, HEIGHT)].reshape(TOKS, DIM), 1, 1)
            row = vocab_iota()
            lab = jnp.sum(jnp.where(row == id_rows(tok_ref, 1, first), logits, 0.0), axis=0, keepdims=True)
            logits = jnp.where(row < VROWS, logits, -1e30)
            top = jnp.max(logits, axis=0, keepdims=True)
            local = top + jnp.log(jnp.sum(jnp.exp(logits - top), axis=0, keepdims=True))
            for t in range(HEIGHT):
                stat[0, pl.ds(first + t, 1), :] = local[:, t * LANE:(t + 1) * LANE]
                stat[0, 32:33, :] = stat[0, 32:33, :] + lab[:, t * LANE:(t + 1) * LANE]

        gather_levels(block, whole, g_send, g_recv, place, forward)
        for lv in range(HEIGHT):
            pl.when(jnp.logical_and(z < TOP, lv <= z))(lambda: sent(lv, 0))
            pl.when(jnp.logical_and(z > 0, lv >= z))(lambda: sent(lv, 1))

        def share(step):
            return remote(stat.at[0], land.at[rank], sem_t, step, z * LEVEL + lax.rem(rank + step, LEVEL))

        for step in range(1, LEVEL):
            share(step).start()
        land[rank] = stat[0]
        for step in range(1, LEVEL):
            share(step).wait()
        stat[1] = merge_stats([land[r] for r in range(LEVEL)])
        for step in range(1, HEIGHT):
            along_z(stat.at[1], land_z.at[z], sem_t, step).start()
        land_z[z] = stat[1]
        for step in range(1, HEIGHT):
            along_z(stat.at[1], land_z.at[z], sem_t, step).wait()
        final = merge_stats([land_z[lv] for lv in range(HEIGHT)])
        lse_ref[...] = final[0:32, :]
        loss_ref[0, 0] = (jnp.sum(final[0:32, :]) - jnp.sum(final[32:STAT, :])) * inv_count

        def backward(first):
            hid = whole[pl.ds(first, HEIGHT)].reshape(TOKS, DIM)
            logits = dot(table[...], hid, 1, 1)
            lse_row = jnp.concatenate([lse_ref[pl.ds(first + t, 1), :] for t in range(HEIGHT)], axis=1)
            row = vocab_iota()
            prob = jnp.exp(jnp.where(row < VROWS, logits, -1e30) - lse_row)
            hit = jnp.where(row == id_rows(tok_ref, 1, first), 1.0, 0.0)
            grad = ((prob - hit) * inv_count).astype(BF16)
            spread[pl.ds(first, HEIGHT)] = dot(grad, table[...], 0, 0).astype(BF16).reshape(HEIGHT, LANE, DIM)
            demb_ref[...] += dot(grad, hid, 1, 0)

        scatter_levels(spread, dhn_ref, ring, place, backward)

        h32 = h_ref[...].astype(F32)
        dh_ref[...] = rms_backward(h32, rms_inv(h32), gain_f, dhn_ref[...])
        mine[...] = dh_ref[...].astype(BF16)
        level_gather(mine, dm_ref, level[HEIGHT], level[5], place)
        for half in range(TWO):
            four = slice(HEIGHT * half, HEIGHT * half + HEIGHT)
            wg, wu = split_weights(gu_ref)
            g = g_ref[half].astype(F32)
            u = u_ref[half].astype(F32)
            dq = dot(dm_ref[four].reshape(TOKS, DIM), wd_ref[...].reshape(UNITS, DIM), 1, 1)
            sig = jax.nn.sigmoid(g)
            dg = (dq * u * sig * (1.0 + g * (1.0 - sig))).astype(BF16)
            du = (dq * g * sig).astype(BF16)
            d_gate[half] = dg
            d_up[half] = du
            parts[four] = (dot(dg, wg, 1, 1) + dot(du, wu, 1, 1)).astype(BF16).reshape(HEIGHT, LANE, DIM)
        def add_slab(dst, srcs):
            def body(i, carry):
                value = srcs[0][i].astype(F32)
                for src in srcs[1:]:
                    value = value + src[i].astype(F32)
                dst[i] = value.astype(dst.dtype)
                return carry
            lax.fori_loop(0, LEVEL, body, 0)

        def hop(lv, way, here=False):
            land = rows_of(land_g, HEIGHT if here and way else lv)
            return remote(rows_of(outgo, lv), land, sem_z, way * HEIGHT + lv, me + LEVEL - CHIPS * way)

        def hop_d(lv, way, here=False):
            return remote(outgo_d.at[lv], land_d.at[HEIGHT if here and way else lv], sem_d, way * HEIGHT + lv, me + LEVEL - CHIPS * way)

        def send(lv, way, more, here):
            @pl.when(more)
            def _():
                hop(lv, way).wait_recv()
                add_slab(rows_of(outgo, lv), [rows_of(ggu, lv), rows_of(land_g, lv)])
                hop_d(lv, way).wait_recv()
                add_into(outgo_d.at[lv], [gd.at[lv], land_d.at[lv]], DROWS)

            @pl.when(jnp.logical_not(more))
            def _():
                add_slab(rows_of(outgo, lv), [rows_of(ggu, lv)])
                add_into(outgo_d.at[lv], [gd.at[lv]], DROWS)
            hop(lv, way, here).start()
            hop_d(lv, way, here).start()

        def send_far(far):
            pl.when(z + far < HEIGHT)(lambda: send(z + far, 0, z > 0, far == 1))
            pl.when(z - far >= 0)(lambda: send(z - far, 1, z < TOP, far == 1))

        def weight_grads():
            for half in range(TWO):
                four = slice(HEIGHT * half, HEIGHT * half + HEIGHT)
                act_in = a_ref[four].reshape(TOKS, DIM)
                news = (dot(act_in, d_gate[half], 0, 0), dot(act_in, d_up[half], 0, 0),
                        dot(acts[half], dm_ref[four].reshape(TOKS, DIM), 0, 0))
                for ref, new in zip((grad_gate, grad_up, grad_down), news):
                    ref[...] = new if half == 0 else ref[...] + new
            both = jnp.concatenate([grad_gate[...].reshape(NDEV, GROWS, UNITS), grad_up[...].reshape(NDEV, GROWS, UNITS)], axis=1)
            ggu[...] = both.astype(BF16)
            gd[...] = grad_down[...].astype(BF16).reshape(WD_SHAPE)

        def grads_off():
            weight_grads()
            send_far(TOP)

        level_scatter(parts, total, *level[:HEIGHT], *level[6:], place, grads_off)
        x = x_ref[...] * emb_scale
        block[...] = (dh_ref[...] + rms_backward(x, rms_inv(x), gain_m, total[...])).astype(BF16)

        demb_ref[...] = demb_ref[...] * (1.0 / emb_scale)

        def add_rows(first):
            demb_ref[...] += dot(hit_rows(first), whole[pl.ds(first, HEIGHT)].reshape(TOKS, DIM), 1, 0)

        def last(way):
            hop(z, way).wait_recv()
            add_slab(acc, [acc, rows_of(land_g, HEIGHT if way else z)])
            hop_d(z, way).wait_recv()
            add_into(dn_ref, [dn_ref, land_d.at[HEIGHT if way else z]], DROWS)

        def give(step):
            peer = lax.rem(rank + step, LEVEL)
            return remote(acc.at[peer], own_ref.at[rank], sem_a, step, z * LEVEL + peer)

        def grads_home():
            add_slab(acc, [rows_of(ggu, z)])
            add_into(dn_ref, [gd.at[z]], DROWS)
            pl.when(z > 0)(lambda: last(0))
            pl.when(z < TOP)(lambda: last(1))
            for step in range(1, LEVEL):
                give(step).start()
            own_ref[rank] = acc[rank]

        def grads_step(t):
            pl.when(t == HEIGHT)(grads_home)

        def grads_late(t):
            pl.when(t == 0)(lambda: send_far(TWO))
            pl.when(t == TWO)(lambda: send_far(1))

        gather_levels(block, whole, g_send, g_recv, place, add_rows, grads_step, grads_late)
        outs = []
        for k in range(LEVEL):
            part = pl.ds(k * LANE, LANE)
            outs.append(pltpu.make_async_copy(demb_ref.at[part], demb_out.at[part], sem_o.at[k]))
        outs.append(pltpu.make_async_copy(dn_ref, dn_out, sem_o.at[LEVEL]))
        for out in outs:
            out.start()
        for step in range(1, LEVEL):
            give(step).wait_recv()
        for step in range(1, LEVEL):
            give(step).wait_send()
        def assemble():
            for k in range(HEIGHT):
                got = jnp.concatenate([own_ref[r, :, DROWS * k:DROWS * (k + 1)] for r in range(LEVEL)], axis=1)
                dgate_ref[:, DIM * k:DIM * (k + 1)] = got[0:GROWS]
                dup_ref[:, DIM * k:DIM * (k + 1)] = got[GROWS:PAIR]

        assemble()
        def gone(lv, way):
            hop(lv, way).wait_send()
            hop_d(lv, way).wait_send()

        for lv in range(HEIGHT):
            pl.when(lv > z)(lambda: gone(lv, 0))
            pl.when(lv < z)(lambda: gone(lv, 1))
        for k, (ref, out) in enumerate(((dgate_ref, dgate_out), (dup_ref, dup_out))):
            outs.append(pltpu.make_async_copy(ref, out, sem_o.at[9 + k]))
            outs[-1].start()
        for out in outs:
            out.wait()

    whole = pltpu.VMEM((NDEV, LANE, DIM), BF16)
    block, flat = pltpu.VMEM((LANE, DIM), BF16), pltpu.VMEM((LANE, DIM), F32)
    slab, slab_d = pltpu.VMEM(GU_SHAPE, BF16), pltpu.VMEM(WD_SHAPE, BF16)
    unit, eight = pltpu.VMEM((TWO, TOKS, UNITS), BF16), pltpu.VMEM((LEVEL, LANE, DIM), BF16)
    wide, tall = pltpu.VMEM((DIM, UNITS), F32), pltpu.VMEM((UNITS, DIM), F32)
    dma = pltpu.SemaphoreType.DMA
    return call(
        kernel, 'step', 0,
        (jax.ShapeDtypeStruct((VPAD, DIM), F32), jax.ShapeDtypeStruct((GROWS, 3072), F32), jax.ShapeDtypeStruct((GROWS, 3072), F32),
         jax.ShapeDtypeStruct((DROWS, DIM), F32), jax.ShapeDtypeStruct((1, 1), F32)),
        (ids, labs, emb, gate, up, down_shard, gain_mlp, gain_final),
        [pltpu.VMEM((VPAD, DIM), F32), pltpu.VMEM((GROWS, 3072), F32), pltpu.VMEM((GROWS, 3072), F32), pltpu.VMEM((DROWS, DIM), F32),
         pltpu.VMEM((VROWS, DIM), BF16), dma((12,)),
         pltpu.VMEM((LEVEL, PAIR, UNITS), BF16), pltpu.VMEM((LEVEL, PAIR, UNITS), F32), pltpu.VMEM((LEVEL, LANE), jnp.int32), pltpu.VMEM((NDEV, LEVEL, LANE), jnp.int32), pltpu.VMEM((VPAD, DIM), BF16), whole, whole,
         slab, slab_d, eight, unit, unit, eight, unit, unit, unit, wide, wide, tall, slab, slab_d,
         pltpu.VMEM((5 * LEVEL, PAIR, UNITS), BF16), pltpu.VMEM((5, DROWS, DIM), BF16), slab, slab_d,
         pltpu.VMEM((LEVEL, PAIR, UNITS), F32), block, flat, block, flat, flat,
         pltpu.VMEM((TWO, STAT, LANE), F32), pltpu.VMEM((LEVEL, STAT, LANE), F32), pltpu.VMEM((HEIGHT, STAT, LANE), F32),
         pltpu.VMEM((32, LANE), F32),
         sem_pair(11), sem_pair(LEVEL), dma((36,)), dma((NDEV,)), sem_pair(LEVEL), sem_pair(LEVEL)]
        + scatter_scratch(LANE, DIM) + LEVEL_SCRATCH)


def solution(mesh):
    group = mesh.shape['fsdp']

    def local_step(ids_blk, lab_blk, emb_shard, gate_shard, up_shard, down_shard, gain_mlp, gain_final):
        emb_scale = math.sqrt(emb_shard.shape[1])
        inv_count = 1.0 / (ids_blk.size * group)
        d_embed, d_gate, d_up, d_down, loss = step_call(
            ids_blk, lab_blk, emb_shard, gate_shard, up_shard, down_shard, gain_mlp, gain_final, emb_scale, inv_count)
        return loss[0, 0], d_embed[0:VROWS] * emb_scale, d_gate, d_up, d_down

    shard_spec = P('fsdp', None)
    return jax.shard_map(local_step, mesh=mesh, in_specs=(shard_spec, shard_spec, shard_spec, shard_spec, shard_spec, shard_spec, P(), P()), out_specs=(P(), shard_spec, shard_spec, shard_spec, shard_spec), check_vma=False)
```

profile of v0, /device:TPU:0, one launch (start us, length us, event | category | flops | bytes accessed | tf_op | source)
XLA Modules:
  0.0 234.7 jit_solution(16063321575796286016)
XLA Ops:
  0.6 226.3 %step.1 = (f32[1024,768]{1,0:T(8,128)}, f32[24,3072]{1,0:T(8,128)}, f32[24,3072]{1,0:T(8,128)}, f32[96,768]{1,0:T(8,128)}, f32[1,1]{1,0:T(1,128)}) custom-call(s32[1,128]{1,0:T(1,128)} %ids_ref.1, s32[1,128]{1,0:T(1,128)} %lab_ref.1, bf16[1004,768]{1,0:T(8,128)(2,1)} %emb_ref.1, bf16[24,3072]{1,0:T(8,128)(2,1)} %gate_ref.1, bf16[24,3072]{1,0:T(8,128)(2,1)} %up_ref.1, ...), custom_call_target="tpu_custom_call" | custom-call | tf_op jit(solution)/shard_map/step/pallas_call | solution.py:447
  226.9 0.0 copy-start.2
  226.9 0.0 copy-start.1
  226.9 0.0 copy-start
  227.0 3.9 %slice_multiply_fusion = f32[1004,768]{1,0:T(8,128)} fusion(f32[1024,768]{1,0:T(8,128)} %get-tuple-element.11), kind=kLoop, calls=%fused_computation | loop fusion | flops 771072 | bytes 6168576 | tf_op jit(solution)/shard_map/mul | solution.py:799
  231.4 0.0 copy-done.2
  231.4 0.7 copy.18
  232.1 0.0 copy-done.1
  232.1 0.7 copy.19
  232.8 0.0 copy-done
  232.8 0.7 copy.20
Async XLA Ops:
  226.9 4.4 %copy-start.2 = (f32[24,3072]{1,0:T(8,128)S(1)}, f32[24,3072]{1,0:T(8,128)}, u32[]{:S(2)}) copy-start(f32[24,3072]{1,0:T(8,128)} %get-tuple-element.22) | copy-start | bytes 884740
  226.9 5.2 %copy-start.1 = (f32[24,3072]{1,0:T(8,128)S(1)}, f32[24,3072]{1,0:T(8,128)}, u32[]{:S(2)}) copy-start(f32[24,3072]{1,0:T(8,128)} %get-tuple-element.23) | copy-start | bytes 884740
  226.9 5.9 %copy-start = (f32[96,768]{1,0:T(8,128)S(1)}, f32[96,768]{1,0:T(8,128)}, u32[]{:S(2)}) copy-start(f32[96,768]{1,0:T(8,128)} %get-tuple-element.24) | copy-start | bytes 884740
where the time goes:
time: 237 us; the launch traced here: 235 us
  Pallas kernels  226 us (95%)
  other arithmetic  3.86 us (2%)
    pallas_call x1, Pallas kernels, call(): pl.pallas_call(kernel, out_shape=outs, in_specs=[VSPEC if i != TWO else H...  226 us

commit v1 on v0

--- a/solution.py
+++ b/solution.py
@@ -697,12 +697,12 @@
         def grads_off():
             weight_grads()
             send_far(TOP)
+            demb_ref[...] = demb_ref[...] * (1.0 / emb_scale)
 
         level_scatter(parts, total, *level[:HEIGHT], *level[6:], place, grads_off)
         x = x_ref[...] * emb_scale
         block[...] = (dh_ref[...] + rms_backward(x, rms_inv(x), gain_m, total[...])).astype(BF16)
 
-        demb_ref[...] = demb_ref[...] * (1.0 / emb_scale)
 
         def add_rows(first):
             demb_ref[...] += dot(hit_rows(first), whole[pl.ds(first, HEIGHT)].reshape(TOKS, DIM), 1, 0)

time: 237 us -> 237 us (level)
  no operation moved by 1% of the time
where the time goes in v1:
time: 237 us; the launch traced here: 235 us
  Pallas kernels  226 us (95%)
  other arithmetic  3.86 us (2%)
    pallas_call x1, Pallas kernels, call(): pl.pallas_call(kernel, out_shape=outs, in_specs=[VSPEC if i != TWO else H...  226 us

profile of v1, /device:TPU:0, one launch (start us, length us, event | category | flops | bytes accessed | tf_op | source)
XLA Modules:
  0.0 234.7 jit_solution(1592890645265258556)
XLA Ops:
  0.6 226.3 %step.1 = (f32[1024,768]{1,0:T(8,128)}, f32[24,3072]{1,0:T(8,128)}, f32[24,3072]{1,0:T(8,128)}, f32[96,768]{1,0:T(8,128)}, f32[1,1]{1,0:T(1,128)}) custom-call(s32[1,128]{1,0:T(1,128)} %ids_ref.1, s32[1,128]{1,0:T(1,128)} %lab_ref.1, bf16[1004,768]{1,0:T(8,128)(2,1)} %emb_ref.1, bf16[24,3072]{1,0:T(8,128)(2,1)} %gate_ref.1, bf16[24,3072]{1,0:T(8,128)(2,1)} %up_ref.1, ...), custom_call_target="tpu_custom_call" | custom-call | tf_op jit(solution)/shard_map/step/pallas_call | solution.py:447
  226.9 0.0 copy-start.2
  226.9 0.0 copy-start.1
  226.9 0.0 copy-start
  227.0 3.9 %slice_multiply_fusion = f32[1004,768]{1,0:T(8,128)} fusion(f32[1024,768]{1,0:T(8,128)} %get-tuple-element.11), kind=kLoop, calls=%fused_computation | loop fusion | flops 771072 | bytes 6168576 | tf_op jit(solution)/shard_map/mul | solution.py:799
  231.4 0.0 copy-done.2
  231.4 0.7 copy.18
  232.1 0.0 copy-done.1
  232.1 0.7 copy.19
  232.8 0.0 copy-done
  232.8 0.7 copy.20
Async XLA Ops:
  226.9 4.4 %copy-start.2 = (f32[24,3072]{1,0:T(8,128)S(1)}, f32[24,3072]{1,0:T(8,128)}, u32[]{:S(2)}) copy-start(f32[24,3072]{1,0:T(8,128)} %get-tuple-element.22) | copy-start | bytes 884740
  226.9 5.2 %copy-start.1 = (f32[24,3072]{1,0:T(8,128)S(1)}, f32[24,3072]{1,0:T(8,128)}, u32[]{:S(2)}) copy-start(f32[24,3072]{1,0:T(8,128)} %get-tuple-element.23) | copy-start | bytes 884740
  226.9 5.9 %copy-start = (f32[96,768]{1,0:T(8,128)S(1)}, f32[96,768]{1,0:T(8,128)}, u32[]{:S(2)}) copy-start(f32[96,768]{1,0:T(8,128)} %get-tuple-element.24) | copy-start | bytes 884740
